TPU v7x, 32 devices: a whole 2x2x4 slice. The times are simulated.
32 devices in a mesh: row: 4 (over z), col: 2 (over y), depth: 4 (over x, core).
Axes of the slice: x: 2, y: 2, z: 4, core: 2. Of those that a mesh axis runs over, the one named last changes fastest.
Arguments:
- a21_leaf: float32 [4, 4096, 2048], P('depth', 'row', 'col'), may hold values from -1.2 to 1.2
- a12_leaf: float32 [4, 2048, 4096], P('depth', 'row', 'col'), may hold values from -1.2 to 1.2
- uinv_leaf: float32 [4, 2048, 2048], P('depth', None, 'col'), may hold values from -0.2 to 1.5, as said below
- linv_leaf: float32 [4, 2048, 2048], P('depth', 'row'), may hold values from -0.2 to 1.5, as said below
- live: int32 [4], P('depth'), may hold values from 16 to 32
- row_map: int32 [4, 32], P('depth', 'row'), may hold values from 0 to 63, as said below
- col_map: int32 [4, 32], P('depth', 'col'), may hold values from 0 to 63, as said below
- a22_anc: float32 [8192, 8192], P(('row', 'depth'), 'col'), may hold values from -6 to 6
- a21_anc: float32 [8192, 2048], P(('row', 'depth'), 'col'), may hold values from -1.2 to 1.2
- a12_anc: float32 [2048, 8192], P(('row', 'depth'), 'col'), may hold values from -1.2 to 1.2
- uinv_anc: float32 [2048, 2048], P(None, 'col'), may hold values from -0.2 to 1.5, as said below
- linv_anc: float32 [2048, 2048], P(('row', 'depth')), may hold values from -0.2 to 1.5, as said below
Outputs:
- leaf_lower: float32 [4, 4096, 2048], P('depth', 'row', 'col')
- leaf_upper: float32 [4, 2048, 4096], P('depth', 'row', 'col')
- anc_lower: float32 [8192, 2048], P(('row', 'depth'), 'col')
- anc_upper: float32 [2048, 8192], P(('row', 'depth'), 'col')
- anc_schur: float32 [8192, 8192], P(('row', 'depth'), 'col')
Inputs may be any that keep to these rules, and one draw needn't show every extreme that they name: `uinv_leaf`: upper triangular: zero below the diagonal, diagonal between 0.5 and 1.5. `linv_leaf`: lower triangular: zero above the diagonal, diagonal between 0.5 and 1.5. `uinv_anc`: upper triangular: zero below the diagonal, diagonal between 0.5 and 1.5. `linv_anc`: lower triangular: zero above the diagonal, diagonal between 0.5 and 1.5. `row_map`: within one replica the entries are distinct. Leaf block row i lies in the k-th of 4 equal ranges of leaf block rows, and its target lies in the k-th of 4 equal ranges of the 64 ancestor block rows. `col_map`: within one replica the entries are distinct. Leaf block column j lies in the k-th of 2 equal ranges of leaf block columns, and its target lies in the k-th of 2 equal ranges of the 64 ancestor block columns.
All inputs are finite; a program needn't handle non-finite values.
Results may differ from a plain program's by a relative error of at most 0.0001.
Values sent between devices are 32-bit elements; how exact they have to be, the bound alone decides.
A program may use at most 256 MiB of HBM per device.

v0:
```python
import jax
import jax.numpy as jnp
from jax import lax
from jax.sharding import PartitionSpec as P

NB = 128


def product(left, right):
    return jnp.dot(left, right, precision=lax.Precision.HIGHEST, preferred_element_type=jnp.float32)


def reduce_depth(update):
    return lax.psum_scatter(update, "depth", scatter_dimension=0, tiled=True)


def combine_depth(schur, row_map, col_map, a22_anc):
    block_size = NB
    rows_here = schur.shape[0]
    cols_here = schur.shape[1]
    leaf_rows = rows_here // block_size
    leaf_cols = cols_here // block_size
    anc_rows = a22_anc.shape[0]
    replicas = lax.axis_size("depth")
    anc_row_blocks = anc_rows * replicas // block_size
    anc_col_blocks = a22_anc.shape[1] // block_size
    row_local = row_map[0] - lax.axis_index("row") * anc_row_blocks
    col_local = col_map[0] - lax.axis_index("col") * anc_col_blocks
    col_pick = (col_local[:, None] == lax.iota(jnp.int32, anc_col_blocks)[None, :]).astype(
        jnp.float32
    )
    row_pick = (row_local[:, None] == lax.iota(jnp.int32, anc_row_blocks)[None, :]).astype(
        jnp.float32
    )
    leaf_blocks = schur.reshape(leaf_rows, block_size, leaf_cols, block_size)
    placed = jnp.einsum("ia,ixjy->axjy", row_pick, leaf_blocks, precision=lax.Precision.HIGHEST)
    placed = jnp.einsum("axjy,jb->axby", placed, col_pick, precision=lax.Precision.HIGHEST)
    update = placed.reshape(anc_row_blocks * block_size, anc_col_blocks * block_size)
    return reduce_depth(update)


def anc_panels(a21_anc, a12_anc, uinv_anc, linv_anc):
    factor = uinv_anc
    anc_lower = product(lax.all_gather(a21_anc, "col", axis=1, tiled=True), factor)
    lower_whole = lax.all_gather(anc_lower, "col", axis=1, tiled=True)
    factor = linv_anc
    anc_upper = product(factor, lax.all_gather(a12_anc, ("row", "depth"), axis=0, tiled=True))
    return (anc_lower, lower_whole, anc_upper)


def shards(
    a21_leaf,
    a12_leaf,
    uinv_leaf,
    linv_leaf,
    live,
    row_map,
    col_map,
    a22_anc,
    a21_anc,
    a12_anc,
    uinv_anc,
    linv_anc,
):
    block_size = NB
    panel_left = a21_leaf[0]
    panel_top = a12_leaf[0]
    upper_inverse = uinv_leaf[0]
    lower_inverse = linv_leaf[0]
    rows_here = panel_left.shape[0]
    cols_here = panel_top.shape[1]
    live_rows = live[0] * block_size
    row_pos = lax.axis_index("row") * rows_here + lax.iota(jnp.int32, rows_here)
    col_pos = lax.axis_index("col") * cols_here + lax.iota(jnp.int32, cols_here)
    row_keep = (row_pos < live_rows).astype(jnp.float32)
    col_keep = (col_pos < live_rows).astype(jnp.float32)
    factor = upper_inverse
    lower_part = product(lax.all_gather(panel_left, "col", axis=1, tiled=True), factor)
    leaf_lower = lower_part * row_keep[:, None]
    factor = lower_inverse
    upper_part = product(factor, lax.all_gather(panel_top, "row", axis=0, tiled=True))
    leaf_upper = upper_part * col_keep[None, :]
    upper_whole = lax.all_gather(leaf_upper, "row", axis=0, tiled=True)
    factor = upper_whole
    schur = jnp.zeros((rows_here, cols_here), jnp.float32) - product(
        lax.all_gather(leaf_lower, "col", axis=1, tiled=True), factor
    )
    own_update = combine_depth(schur, row_map, col_map, a22_anc)
    anc_lower, lower_whole, anc_upper = anc_panels(a21_anc, a12_anc, uinv_anc, linv_anc)
    factor = lower_whole
    anc_schur = (
        a22_anc
        + own_update
        - product(factor, lax.all_gather(anc_upper, ("row", "depth"), axis=0, tiled=True))
    )
    return (leaf_lower[None], leaf_upper[None], anc_lower, anc_upper, anc_schur)


def solution(mesh):
    in_specs = (
        P("depth", "row", "col"),
        P("depth", "row", "col"),
        P("depth", None, "col"),
        P("depth", "row", None),
        P("depth"),
        P("depth", "row"),
        P("depth", "col"),
        P(("row", "depth"), "col"),
        P(("row", "depth"), "col"),
        P(("row", "depth"), "col"),
        P(None, "col"),
        P(("row", "depth"), None),
    )
    out_specs = (
        P("depth", "row", "col"),
        P("depth", "row", "col"),
        P(("row", "depth"), "col"),
        P(("row", "depth"), "col"),
        P(("row", "depth"), "col"),
    )
    return jax.shard_map(shards, mesh=mesh, in_specs=in_specs, out_specs=out_specs, check_vma=False)
```

profile of v0, /device:TPU:0, one launch (start us, length us, event | category | flops | bytes accessed | tf_op | source)
XLA Modules:
  0.0 1554.8 jit_solution(6377144033500188488)
XLA Ops:
  7.2 0.0 copy-start
  7.2 0.0 all-gather.23.cloned.1.call-start
  7.2 0.7 all-gather.23.cloned.1.call-update
  7.9 0.0 all-gather.25.cloned.1.call-start
  8.0 0.7 all-gather.25.cloned.1.call-update
  8.7 0.0 all-gather.11.cloned.1.call-start
  8.7 0.7 all-gather.11.cloned.1.call-update
  9.4 0.0 all-gather.15.cloned.1.call-start
  10.1 106.2 %all-gather.23.cloned.1.call-done = f32[1,1024,2048]{2,1,0:T(8,128)} async-done(((f32[1,1024,1024]{2,1,0:T(8,128)}), f32[1,1024,2048]{2,1,0:T(8,128)}) %all-gather.23.cloned.1.call-update) | async-done | bytes 8388624 | tf_op jit(solution)/shard_map/all_gather | solution.py:78
  116.3 31.9 %fusion.15 = f32[1024,1024]{1,0:T(8,128)} fusion(f32[1,2048,1024]{2,1,0:T(8,128)} %param.14, f32[1,1024,2048]{2,1,0:T(8,128)} %all-gather.23.cloned.1.call-done, f32[1024]{0:T(1024)S(1)} %fusion.24), kind=kOutput, calls=%fused_computation.14 | convolution fusion | flops 25770852352 | bytes 20975616 | tf_op jit(solution)/shard_map/dot_general | solution.py:10
  148.1 0.0 all-gather.15.cloned.1.call-update
  148.2 0.0 all-gather.17.cloned.1.call-start
  148.2 0.0 copy-start.1
  148.2 0.0 copy-start.2
  148.3 256.4 %all-gather.25.cloned.1.call-done = f32[1,2048,2048]{2,1,0:T(8,128)} async-done(((f32[1,512,2048]{2,1,0:T(8,128)}), f32[1,2048,2048]{2,1,0:T(8,128)}) %all-gather.25.cloned.1.call-update) | async-done | bytes 16777232 | tf_op jit(solution)/shard_map/all_gather | solution.py:81
  404.6 32.8 %fusion.10 = f32[512,2048]{1,0:T(8,128)} fusion(f32[1,2048,2048]{2,1,0:T(8,128)} %all-gather.25.cloned.1.call-done, f32[1,512,2048]{2,1,0:T(8,128)} %param.15, f32[2048]{0:T(1024)S(1)} %fusion.20), kind=kOutput, calls=%fused_computation.13 | convolution fusion | flops 25770852352 | bytes 25174016 | tf_op jit(solution)/shard_map/dot_general | solution.py:10
  437.5 0.0 all-gather.17.cloned.1.call-update
  437.5 0.0 all-gather.13.cloned.1.call-start
  437.5 0.5 all-gather.13.cloned.1.call-update
  438.1 0.3 all-gather.19.cloned.1.call-start
  438.4 0.0 copy-done.1
  438.4 0.0 copy-done.2
  438.4 22.7 %all-gather.11.cloned.1.call-done = f32[512,2048]{1,0:T(8,128)} async-done(((f32[512,1024]{1,0:T(8,128)}), f32[512,2048]{1,0:T(8,128)}) %all-gather.11.cloned.1.call-update) | async-done | bytes 4194320 | tf_op jit(solution)/shard_map/all_gather | solution.py:44
  461.1 17.5 %fusion.28 = f32[512,1024]{1,0:T(8,128)} fusion(f32[512,2048]{1,0:T(8,128)} %all-gather.11.cloned.1.call-done, f32[2048,1024]{1,0:T(8,128)} %param.22), kind=kOutput, calls=%fused_computation.27 | convolution fusion | flops 12884901888 | bytes 14680064 | tf_op jit(solution)/shard_map/dot_general | solution.py:10
  478.7 0.0 all-gather.19.cloned.1.call-update
  478.7 0.0 reduce-scatter.2.cloned.1.call-start
  478.7 88.4 %all-gather.15.cloned.1.call-done = f32[1024,2048]{1,0:T(8,128)} async-done(((f32[1024,1024]{1,0:T(8,128)}), f32[1024,2048]{1,0:T(8,128)}) %all-gather.15.cloned.1.call-update) | async-done | bytes 8388624 | tf_op jit(solution)/shard_map/all_gather | solution.py:86
  567.1 288.8 %all-gather.17.cloned.1.call-done = f32[2048,2048]{1,0:T(8,128)} async-done(((f32[512,2048]{1,0:T(8,128)}), f32[2048,2048]{1,0:T(8,128)}) %all-gather.17.cloned.1.call-update) | async-done | bytes 16777232 | tf_op jit(solution)/shard_map/all_gather | solution.py:83
  855.9 69.7 %subtract_bitcast_fusion = f32[128,8,16,128]{3,1,2,0:T(8,128)S(1)} fusion(f32[1024,2048]{1,0:T(8,128)} %all-gather.15.cloned.1.call-done, f32[2048,2048]{1,0:T(8,128)} %all-gather.17.cloned.1.call-done), kind=kOutput, calls=%fused_computation.11 | convolution fusion | flops 51541704704 | bytes 33554432 | tf_op jit(solution)/shard_map/dot_general | solution.py:10
  925.6 2.0 copy.21
  927.6 9.7 fusion.7
  937.4 21.8 %fusion.2 = f32[32,16,128,128]{3,0,2,1:T(8,128)} fusion(f32[16,128,16,128]{3,0,2,1:T(8,128)S(1)} %fusion.7, s32[16]{0:T(128)S(1)} %subtract_bitcast_fusion.2), kind=kOutput, calls=%fused_computation.3 | convolution fusion | flops 1610613248 | bytes 50331712 | tf_op jit(solution)/shard_map/axjy,jb->axby/dot_general | solution.py:37
  959.2 38.4 %copy.28 = f32[256,8,32,128]{3,1,2,0:T(8,128)} copy(f32[256,8,32,128]{3,2,1,0:T(8,128)} %bitcast.56) | data formatting | bytes 67108864
  997.5 0.0 reduce-scatter.2.cloned.1.call-update
  997.5 0.0 all-gather.21.cloned.1.call-start
  997.6 26.0 %all-gather.13.cloned.1.call-done = f32[2048,4096]{1,0:T(8,128)} async-done(((f32[128,4096]{1,0:T(8,128)}), f32[2048,4096]{1,0:T(8,128)}) %all-gather.13.cloned.1.call-update) | async-done | bytes 33554448 | tf_op jit(solution)/shard_map/all_gather | solution.py:47
  1023.6 0.0 copy-done
  1023.6 22.6 %fusion.29 = f32[128,4096]{1,0:T(8,128)} fusion(f32[128,2048]{1,0:T(8,128)S(1)} %copy-done, f32[2048,4096]{1,0:T(8,128)} %all-gather.13.cloned.1.call-done), kind=kOutput, calls=%fused_computation.28 | convolution fusion | flops 12884901888 | bytes 36700160 | tf_op jit(solution)/shard_map/dot_general | solution.py:10
  1046.1 0.0 all-gather.21.cloned.1.call-update
  1046.2 36.3 %all-gather.19.cloned.1.call-done = f32[512,2048]{1,0:T(8,128)} async-done(((f32[512,1024]{1,0:T(8,128)}), f32[512,2048]{1,0:T(8,128)}) %all-gather.19.cloned.1.call-update) | async-done | bytes 4194320 | tf_op jit(solution)/shard_map/all_gather | solution.py:45
  1082.4 234.9 %reduce-scatter.2.cloned.1.call-done = f32[512,4096]{1,0:T(8,128)} async-done(((f32[2048,4096]{1,0:T(8,128)}), f32[512,4096]{1,0:T(8,128)}) %reduce-scatter.2.cloned.1.call-update) | async-done | bytes 8388624 | tf_op jit(solution)/shard_map/reduce_scatter | solution.py:14
  1317.4 170.3 %all-gather.21.cloned.1.call-done = f32[2048,4096]{1,0:T(8,128)} async-done(((f32[128,4096]{1,0:T(8,128)}), f32[2048,4096]{1,0:T(8,128)}) %all-gather.21.cloned.1.call-update) | async-done | bytes 33554448 | tf_op jit(solution)/shard_map/all_gather | solution.py:94
  1487.6 60.3 %add_subtract_fusion = f32[512,4096]{1,0:T(8,128)} fusion(f32[512,4096]{1,0:T(8,128)} %param.19, f32[512,4096]{1,0:T(8,128)} %reduce-scatter.2.cloned.1.call-done, f32[512,2048]{1,0:T(8,128)} %all-gather.19.cloned.1.call-done, f32[2048,4096]{1,0:T(8,128)} %all-gather.21.cloned.1.call-done), kind=kOutput, calls=%fused_computation.10 | convolution fusion | flops 51543801856 | bytes 62914560 | tf_op jit(solution)/shard_map/dot_general | solution.py:10
  (4 shorter events, 0.0 us)
Async XLA Ops:
  7.2 1016.4 %copy-start = (f32[128,2048]{1,0:T(8,128)S(1)}, f32[128,2048]{1,0:T(8,128)}, u32[]{:S(2)}) copy-start(f32[128,2048]{1,0:T(8,128)} %param.23) | copy-start | bytes 3145732
  7.2 109.1 %all-gather.23.cloned.1.call-start = ((), (), s32[]{:S(2)}) async-start(), calls=%async_computation.8 | async-start | bytes 12582912 | tf_op jit(solution)/shard_map/all_gather | solution.py:78
  7.9 396.7 %all-gather.25.cloned.1.call-start = ((), (), s32[]{:S(2)}) async-start(), calls=%async_computation.9 | async-start | bytes 20971520 | tf_op jit(solution)/shard_map/all_gather | solution.py:81
  8.7 452.5 %all-gather.11.cloned.1.call-start = ((), (), s32[]{:S(2)}) async-start(), calls=%async_computation.1 | async-start | bytes 6291456 | tf_op jit(solution)/shard_map/all_gather | solution.py:44
  9.4 557.7 %all-gather.15.cloned.1.call-start = ((), (), s32[]{:S(2)}) async-start(), calls=%async_computation.3 | async-start | bytes 12582912 | tf_op jit(solution)/shard_map/all_gather | solution.py:86
  148.2 707.7 %all-gather.17.cloned.1.call-start = ((), (), s32[]{:S(2)}) async-start(), calls=%async_computation.4 | async-start | bytes 20971520 | tf_op jit(solution)/shard_map/all_gather | solution.py:83
  148.2 290.1 %copy-start.1 = (s32[1,8]{1,0:T(1,128)S(1)}, s32[1,8]{1,0:T(1,128)}, u32[]{:S(2)}) copy-start(s32[1,8]{1,0:T(1,128)} %param.17) | copy-start | bytes 100
  148.2 290.1 %copy-start.2 = (s32[1,16]{1,0:T(1,128)S(1)}, s32[1,16]{1,0:T(1,128)}, u32[]{:S(2)}) copy-start(s32[1,16]{1,0:T(1,128)} %param.18) | copy-start | bytes 196
  437.5 586.1 %all-gather.13.cloned.1.call-start = ((), (), s32[]{:S(2)}) async-start(), calls=%async_computation.2 | async-start | bytes 35651584 | tf_op jit(solution)/shard_map/all_gather | solution.py:47
  438.1 644.4 %all-gather.19.cloned.1.call-start = ((), (), s32[]{:S(2)}) async-start(), calls=%async_computation.6 | async-start | bytes 6291456 | tf_op jit(solution)/shard_map/all_gather | solution.py:45
  478.7 838.7 %reduce-scatter.2.cloned.1.call-start = ((), (), s32[]{:S(2)}) async-start(), calls=%async_computation.5 | async-start | bytes 41943040 | tf_op jit(solution)/shard_map/reduce_scatter | solution.py:14
  997.5 490.1 %all-gather.21.cloned.1.call-start = ((), (), s32[]{:S(2)}) async-start(), calls=%async_computation.7 | async-start | bytes 35651584 | tf_op jit(solution)/shard_map/all_gather | solution.py:94
Sparse Core Ops, SparseCore 0:
  9.5 106.6 all-gather.22
  117.8 286.7 all-gather.24
  406.2 54.8 all-gather.10
  463.1 103.9 all-gather.14
  569.1 286.7 all-gather.16
  857.3 166.2 all-gather.12
  1025.7 56.6 all-gather.18
  1085.0 232.3 reduce-scatter.1
  1319.6 168.0 all-gather.20
where the time goes:
time: 1560 us; the launch traced here: 1550 us
  waiting for transfers between devices  1230 us (79%)
  matrix products  266 us (17%)
  local copies, waits for them, and re-layouts  40.4 us (3%)
    all_gather x1, waiting for transfers between devices, shards(): upper_whole = lax.all_gather(leaf_upper, 'row', axis=0, tiled=True)  289 us
    all_gather x1, waiting for transfers between devices, shards(): lax.all_gather(panel_top, 'row', axis=0, tiled=True)  256 us
    reduce_scatter x1, waiting for transfers between devices, reduce_depth(): return lax.psum_scatter(update, 'depth', scatter_dimension=0, tiled=True)  235 us
    dot_general x6, matrix products, product(): jnp.dot(left, right, precision=lax.Precision.HIGHEST, preferred_element_t...  235 us
    all_gather x1, waiting for transfers between devices, shards(): lax.all_gather(anc_upper, ('row', 'depth'), axis=0, tiled=True)  170 us
    all_gather x1, waiting for transfers between devices, shards(): lax.all_gather(panel_left, 'col', axis=1, tiled=True)  106 us
    all_gather x1, waiting for transfers between devices, shards(): lax.all_gather(leaf_lower, 'col', axis=1, tiled=True)  88.4 us
    unnamed x8, local copies, waits for them, and re-layouts  40.4 us
  transfers between devices with their start and end apart: 9, of which 9 were waited for; matrix products, arithmetic and copies ran while one was open for 16% of the time, Pallas kernels for 0%

commit v1 on v0

--- a/solution.py
+++ b/solution.py
@@ -83,7 +83,7 @@
     upper_whole = lax.all_gather(leaf_upper, "row", axis=0, tiled=True)
     factor = upper_whole
     schur = jnp.zeros((rows_here, cols_here), jnp.float32) - product(
-        lax.all_gather(leaf_lower, "col", axis=1, tiled=True), factor
+        jnp.concatenate(lax.all_gather(leaf_lower, "col"), axis=1), factor
     )
     own_update = combine_depth(schur, row_map, col_map, a22_anc)
     anc_lower, lower_whole, anc_upper = anc_panels(a21_anc, a12_anc, uinv_anc, linv_anc)

time: 1560 us -> 1560 us (level)
  transfers between devices with their start and end apart: 9 -> 9, of which waited for: 9 -> 9; matrix products, arithmetic and copies ran while one was open for 16% -> 17% of each run, Pallas kernels for 0% -> 0%
where the time goes in v1:
time: 1560 us; the launch traced here: 1550 us
  waiting for transfers between devices  1220 us (78%)
  matrix products  269 us (17%)
  local copies, waits for them, and re-layouts  48.9 us (3%)
    all_gather x1, waiting for transfers between devices, shards(): upper_whole = lax.all_gather(leaf_upper, 'row', axis=0, tiled=True)  280 us
    all_gather x1, waiting for transfers between devices, shards(): lax.all_gather(panel_top, 'row', axis=0, tiled=True)  256 us
    dot_general x6, matrix products, product(): jnp.dot(left, right, precision=lax.Precision.HIGHEST, preferred_element_t...  238 us
    reduce_scatter x1, waiting for transfers between devices, reduce_depth(): return lax.psum_scatter(update, 'depth', scatter_dimension=0, tiled=True)  235 us
    all_gather x1, waiting for transfers between devices, shards(): lax.all_gather(anc_upper, ('row', 'depth'), axis=0, tiled=True)  170 us
    all_gather x1, waiting for transfers between devices, shards(): lax.all_gather(panel_left, 'col', axis=1, tiled=True)  106 us
    all_gather x1, waiting for transfers between devices, shards(): lax.all_gather(leaf_lower, 'col')  88.4 us
    unnamed x8, local copies, waits for them, and re-layouts  40.2 us
  transfers between devices with their start and end apart: 9, of which 9 were waited for; matrix products, arithmetic and copies ran while one was open for 17% of the time, Pallas kernels for 0%

profile of v1, /device:TPU:0, one launch (start us, length us, event | category | flops | bytes accessed | tf_op | source)
XLA Modules:
  0.0 1554.8 jit_solution(6031711031553715772)
XLA Ops:
  7.2 0.0 copy-start
  7.2 0.0 all-gather.22.cloned.1.call-start
  7.2 0.7 all-gather.22.cloned.1.call-update
  7.9 0.0 all-gather.24.cloned.1.call-start
  8.0 0.7 all-gather.24.cloned.1.call-update
  8.7 0.0 all-gather.12.cloned.1.call-start
  8.7 0.7 all-gather.12.cloned.1.call-update
  9.4 0.0 all-gather.26.cloned.1.call-start
  10.1 106.2 %all-gather.22.cloned.1.call-done = f32[1,1024,2048]{2,1,0:T(8,128)} async-done(((f32[1,1024,1024]{2,1,0:T(8,128)}), f32[1,1024,2048]{2,1,0:T(8,128)}) %all-gather.22.cloned.1.call-update) | async-done | bytes 8388624 | tf_op jit(solution)/shard_map/all_gather | solution.py:78
  116.3 31.9 %fusion.15 = f32[1024,1024]{1,0:T(8,128)} fusion(f32[1,2048,1024]{2,1,0:T(8,128)} %param.14, f32[1,1024,2048]{2,1,0:T(8,128)} %all-gather.22.cloned.1.call-done, f32[1024]{0:T(1024)S(1)} %fusion.24), kind=kOutput, calls=%fused_computation.14 | convolution fusion | flops 25770852352 | bytes 20975616 | tf_op jit(solution)/shard_map/dot_general | solution.py:10
  148.1 0.0 all-gather.26.cloned.1.call-update
  148.2 0.0 all-gather.16.cloned.1.call-start
  148.2 0.0 copy-start.1
  148.2 0.0 copy-start.2
  148.3 256.4 %all-gather.24.cloned.1.call-done = f32[1,2048,2048]{2,1,0:T(8,128)} async-done(((f32[1,512,2048]{2,1,0:T(8,128)}), f32[1,2048,2048]{2,1,0:T(8,128)}) %all-gather.24.cloned.1.call-update) | async-done | bytes 16777232 | tf_op jit(solution)/shard_map/all_gather | solution.py:81
  404.6 32.8 %fusion.10 = f32[512,2048]{1,0:T(8,128)} fusion(f32[1,2048,2048]{2,1,0:T(8,128)} %all-gather.24.cloned.1.call-done, f32[1,512,2048]{2,1,0:T(8,128)} %param.15, f32[2048]{0:T(1024)S(1)} %fusion.20), kind=kOutput, calls=%fused_computation.13 | convolution fusion | flops 25770852352 | bytes 25174016 | tf_op jit(solution)/shard_map/dot_general | solution.py:10
  437.5 0.0 all-gather.16.cloned.1.call-update
  437.5 0.0 all-gather.14.cloned.1.call-start
  437.5 0.5 all-gather.14.cloned.1.call-update
  438.1 0.3 all-gather.18.cloned.1.call-start
  438.4 0.0 copy-done.1
  438.4 0.0 copy-done.2
  438.4 22.7 %all-gather.12.cloned.1.call-done = f32[512,2048]{1,0:T(8,128)} async-done(((f32[512,1024]{1,0:T(8,128)}), f32[512,2048]{1,0:T(8,128)}) %all-gather.12.cloned.1.call-update) | async-done | bytes 4194320 | tf_op jit(solution)/shard_map/all_gather | solution.py:44
  461.1 17.5 %fusion.28 = f32[512,1024]{1,0:T(8,128)} fusion(f32[512,2048]{1,0:T(8,128)} %all-gather.12.cloned.1.call-done, f32[2048,1024]{1,0:T(8,128)} %param.22), kind=kOutput, calls=%fused_computation.27 | convolution fusion | flops 12884901888 | bytes 14680064 | tf_op jit(solution)/shard_map/dot_general | solution.py:10
  478.7 0.0 all-gather.18.cloned.1.call-update
  478.7 0.0 reduce-scatter.2.cloned.1.call-start
  478.7 88.4 %all-gather.26.cloned.1.call-done = f32[2048,1024]{1,0:T(8,128)} async-done(((f32[1024,1024]{1,0:T(8,128)}), f32[2048,1024]{1,0:T(8,128)}) %all-gather.26.cloned.1.call-update) | async-done | bytes 8388624 | tf_op jit(solution)/shard_map/all_gather | solution.py:86
  567.1 8.7 copy.17
  575.8 280.1 %all-gather.16.cloned.1.call-done = f32[2048,2048]{1,0:T(8,128)} async-done(((f32[512,2048]{1,0:T(8,128)}), f32[2048,2048]{1,0:T(8,128)}) %all-gather.16.cloned.1.call-update) | async-done | bytes 16777232 | tf_op jit(solution)/shard_map/all_gather | solution.py:83
  855.9 72.9 %subtract_bitcast_fusion = f32[128,8,16,128]{3,1,2,0:T(8,128)S(1)} fusion(f32[1024,2048]{0,1:T(8,128)} %bitcast.63, f32[2048,2048]{1,0:T(8,128)} %all-gather.16.cloned.1.call-done), kind=kOutput, calls=%fused_computation.11 | convolution fusion | flops 51541704704 | bytes 33554432 | tf_op jit(solution)/shard_map/dot_general | solution.py:10
  928.8 2.0 copy.22
  930.8 9.7 fusion.7
  940.5 21.8 %fusion.2 = f32[32,16,128,128]{3,0,2,1:T(8,128)} fusion(f32[16,128,16,128]{3,0,2,1:T(8,128)S(1)} %fusion.7, s32[16]{0:T(128)S(1)} %subtract_bitcast_fusion.2), kind=kOutput, calls=%fused_computation.3 | convolution fusion | flops 1610613248 | bytes 50331712 | tf_op jit(solution)/shard_map/axjy,jb->axby/dot_general | solution.py:37
  962.3 38.2 %copy.29 = f32[256,8,32,128]{3,1,2,0:T(8,128)} copy(f32[256,8,32,128]{3,2,1,0:T(8,128)} %bitcast.60) | data formatting | bytes 67108864
  1000.5 0.0 reduce-scatter.2.cloned.1.call-update
  1000.5 0.0 all-gather.20.cloned.1.call-start
  1000.6 23.0 %all-gather.14.cloned.1.call-done = f32[2048,4096]{1,0:T(8,128)} async-done(((f32[128,4096]{1,0:T(8,128)}), f32[2048,4096]{1,0:T(8,128)}) %all-gather.14.cloned.1.call-update) | async-done | bytes 33554448 | tf_op jit(solution)/shard_map/all_gather | solution.py:47
  1023.6 0.0 copy-done
  1023.6 22.6 %fusion.29 = f32[128,4096]{1,0:T(8,128)} fusion(f32[128,2048]{1,0:T(8,128)S(1)} %copy-done, f32[2048,4096]{1,0:T(8,128)} %all-gather.14.cloned.1.call-done), kind=kOutput, calls=%fused_computation.28 | convolution fusion | flops 12884901888 | bytes 36700160 | tf_op jit(solution)/shard_map/dot_general | solution.py:10
  1046.2 0.0 all-gather.20.cloned.1.call-update
  1046.2 36.3 %all-gather.18.cloned.1.call-done = f32[512,2048]{1,0:T(8,128)} async-done(((f32[512,1024]{1,0:T(8,128)}), f32[512,2048]{1,0:T(8,128)}) %all-gather.18.cloned.1.call-update) | async-done | bytes 4194320 | tf_op jit(solution)/shard_map/all_gather | solution.py:45
  1082.5 234.9 %reduce-scatter.2.cloned.1.call-done = f32[512,4096]{1,0:T(8,128)} async-done(((f32[2048,4096]{1,0:T(8,128)}), f32[512,4096]{1,0:T(8,128)}) %reduce-scatter.2.cloned.1.call-update) | async-done | bytes 8388624 | tf_op jit(solution)/shard_map/reduce_scatter | solution.py:14
  1317.4 170.3 %all-gather.20.cloned.1.call-done = f32[2048,4096]{1,0:T(8,128)} async-done(((f32[128,4096]{1,0:T(8,128)}), f32[2048,4096]{1,0:T(8,128)}) %all-gather.20.cloned.1.call-update) | async-done | bytes 33554448 | tf_op jit(solution)/shard_map/all_gather | solution.py:94
  1487.6 60.3 %add_subtract_fusion = f32[512,4096]{1,0:T(8,128)} fusion(f32[512,4096]{1,0:T(8,128)} %param.19, f32[512,4096]{1,0:T(8,128)} %reduce-scatter.2.cloned.1.call-done, f32[512,2048]{1,0:T(8,128)} %all-gather.18.cloned.1.call-done, f32[2048,4096]{1,0:T(8,128)} %all-gather.20.cloned.1.call-done), kind=kOutput, calls=%fused_computation.10 | convolution fusion | flops 51543801856 | bytes 62914560 | tf_op jit(solution)/shard_map/dot_general | solution.py:10
  (4 shorter events, 0.0 us)
Async XLA Ops:
  7.2 1016.4 %copy-start = (f32[128,2048]{1,0:T(8,128)S(1)}, f32[128,2048]{1,0:T(8,128)}, u32[]{:S(2)}) copy-start(f32[128,2048]{1,0:T(8,128)} %param.23) | copy-start | bytes 3145732
  7.2 109.1 %all-gather.22.cloned.1.call-start = ((), (), s32[]{:S(2)}) async-start(), calls=%async_computation.7 | async-start | bytes 12582912 | tf_op jit(solution)/shard_map/all_gather | solution.py:78
  7.9 396.7 %all-gather.24.cloned.1.call-start = ((), (), s32[]{:S(2)}) async-start(), calls=%async_computation.8 | async-start | bytes 20971520 | tf_op jit(solution)/shard_map/all_gather | solution.py:81
  8.7 452.5 %all-gather.12.cloned.1.call-start = ((), (), s32[]{:S(2)}) async-start(), calls=%async_computation.1 | async-start | bytes 6291456 | tf_op jit(solution)/shard_map/all_gather | solution.py:44
  9.4 557.7 %all-gather.26.cloned.1.call-start = ((), (), s32[]{:S(2)}) async-start(), calls=%async_computation.9 | async-start | bytes 12582912 | tf_op jit(solution)/shard_map/all_gather | solution.py:86
  148.2 707.7 %all-gather.16.cloned.1.call-start = ((), (), s32[]{:S(2)}) async-start(), calls=%async_computation.3 | async-start | bytes 20971520 | tf_op jit(solution)/shard_map/all_gather | solution.py:83
  148.2 290.1 %copy-start.1 = (s32[1,8]{1,0:T(1,128)S(1)}, s32[1,8]{1,0:T(1,128)}, u32[]{:S(2)}) copy-start(s32[1,8]{1,0:T(1,128)} %param.17) | copy-start | bytes 100
  148.2 290.1 %copy-start.2 = (s32[1,16]{1,0:T(1,128)S(1)}, s32[1,16]{1,0:T(1,128)}, u32[]{:S(2)}) copy-start(s32[1,16]{1,0:T(1,128)} %param.18) | copy-start | bytes 196
  437.5 586.1 %all-gather.14.cloned.1.call-start = ((), (), s32[]{:S(2)}) async-start(), calls=%async_computation.2 | async-start | bytes 35651584 | tf_op jit(solution)/shard_map/all_gather | solution.py:47
  438.1 644.4 %all-gather.18.cloned.1.call-start = ((), (), s32[]{:S(2)}) async-start(), calls=%async_computation.5 | async-start | bytes 6291456 | tf_op jit(solution)/shard_map/all_gather | solution.py:45
  478.7 838.7 %reduce-scatter.2.cloned.1.call-start = ((), (), s32[]{:S(2)}) async-start(), calls=%async_computation.4 | async-start | bytes 41943040 | tf_op jit(solution)/shard_map/reduce_scatter | solution.py:14
  1000.5 487.1 %all-gather.20.cloned.1.call-start = ((), (), s32[]{:S(2)}) async-start(), calls=%async_computation.6 | async-start | bytes 35651584 | tf_op jit(solution)/shard_map/all_gather | solution.py:94
Sparse Core Ops, SparseCore 0:
  9.5 106.6 all-gather.21
  117.8 286.7 all-gather.23
  406.2 54.8 all-gather.11
  463.1 103.9 all-gather.25
  569.1 286.7 all-gather.15
  857.3 166.2 all-gather.13
  1025.7 56.6 all-gather.17
  1085.0 232.3 reduce-scatter.1
  1319.6 168.0 all-gather.19
